TPU v7x, 256 devices: a whole 4x4x8 slice. The times are simulated.
256 devices in a mesh: expert: 4 (over y), shard: 64 (over z, x, core).
Axes of the slice: x: 4, y: 4, z: 8, core: 2. Of those that a mesh axis runs over, the one named last changes fastest.
Arguments:
- gradient: bfloat16 [4, 2048, 28672], P('expert', 'shard'), may hold values from -16 to 16
- factor: float32 [4, 2048, 512], P('expert', 'shard'), may hold values from -2 to 2, as said below
- right_diag: float32 [4, 28672], P('expert', 'shard'), may hold values from 0.5 to 2
- counts: int32 [4], P('expert'), may hold values from 256 to 1023
Outputs:
- new_factor: float32 [4, 2048, 512], P('expert', 'shard')
- new_right: float32 [4, 28672], P('expert', 'shard')
Inputs may be any that keep to these rules, and one draw needn't show every extreme that they name: Every diagonal block of factor is upper triangular with a positive diagonal: in row r, entry j is zero for j < r % 512.
All inputs are finite; a program needn't handle non-finite values. Where the computation divides by a largest or mean magnitude, that divisor is 1e-20 or more.
Results may differ from a plain program's by a relative error of at most 0.002.
Values may be sent and summed in bfloat16 or wider, within the bound.
No kernel may reach another device: no remote copies, remote signals or barrier semaphores. Data moves between devices by JAX's collectives and lax.ppermute only.
A program may use at most 128 MiB of HBM per device.

v0:
```python
import jax
import jax.numpy as jnp
from jax import lax
from jax.sharding import Mesh
from jax.sharding import PartitionSpec as P

FF = 14336
SHARD = ("shard_0", "shard_1", "shard_2")
step_rate = 0.5
epsilon = 1e-06


def from_everyone(shard, axis):
    size = lax.axis_size(axis)
    return lax.all_to_all(
        jnp.broadcast_to(shard[None], (size, *shard.shape)), axis, 0, 0, tiled=True
    )


def of_everyone(shard, axis):
    everything = from_everyone(shard, axis)
    return jnp.sum(everything, axis=0)


def cut_along(shard, dim, size):
    before, after = (shard.shape[:dim], shard.shape[dim + 1 :])
    return jnp.moveaxis(shard.reshape(*before, size, -1, *after), dim, 0)


def laid_out(parts, dim):
    shape = list(parts.shape[1:])
    shape[dim] *= parts.shape[0]
    return jnp.moveaxis(parts, 0, dim).reshape(shape)


def moved_by_axis(parts, axes, sequence):
    inside = parts.shape[1:]
    out = parts.reshape(*(lax.axis_size(a) for a in axes), *inside)
    for k in sequence:
        out = lax.all_to_all(out, axes[k], k, k, tiled=True)
    return out.reshape(-1, *inside)


def two_step_exchange(shard, groups, sequence, split_dim, concat_dim):
    size = lax.axis_size(groups[0]) * lax.axis_size(groups[1])
    parts = cut_along(shard, split_dim, size)
    return laid_out(moved_by_axis(parts, groups, sequence), concat_dim)


def all_blocks(shard, axes, sequence):
    parts = shard[None]
    for k in sequence:
        parts = lax.all_gather(parts, axes[k], axis=0, tiled=True)
    held = [lax.axis_size(axes[k]) for k in reversed(sequence)]
    parts = parts.reshape(*held, *shard.shape)
    turned = sorted(range(len(sequence)), key=lambda place: sequence[len(sequence) - 1 - place])
    return parts.transpose(*turned, *range(len(sequence), parts.ndim)).reshape(-1, *shard.shape)


def gather_axes(shard, axes, sequence, dim):
    return laid_out(all_blocks(shard, axes, sequence), dim)


def sum_by_axis(so_far, axes):
    for axis in axes:
        so_far = lax.psum_scatter(so_far, axis, scatter_dimension=0, tiled=True)
    return so_far


def of_everyone_2(shard, axis):
    return from_everyone(shard, axis).max(axis=0)


def in_one(arrays, axis):
    ends = [0]
    for a in arrays:
        ends.append(ends[-1] + a.size)
    so_far = of_everyone_2(jnp.concatenate([a.ravel() for a in arrays]), axis)
    return tuple((so_far[b:e].reshape(a.shape) for a, b, e in zip(arrays, ends, ends[1:])))


def body(gradient, factor, right_diag, counts):
    local_experts = counts.shape[0]
    experts_all = local_experts * lax.axis_size("expert")
    token_sum = of_everyone(jnp.sum(counts), "expert")
    weight = experts_all * counts.astype(jnp.float32) / jnp.asarray(token_sum).astype(jnp.float32)
    squared = weight * weight
    columns = two_step_exchange(gradient, (("shard_0", "shard_1"), "shard_2"), (1, 0), 2, 1)
    own_rows = factor.shape[1]
    block = factor.shape[2]
    width = columns.shape[1]
    col_count = columns.shape[2]
    narrow = factor.astype(jnp.bfloat16)
    whole = gather_axes(narrow, SHARD, (1, 0, 2), 1)
    blocks = width // block
    left = whole.reshape((local_experts, blocks, block, block))
    right = columns.reshape((local_experts, blocks, block, col_count))
    raw = jnp.einsum("ebik,ebkc->ebic", left, right, preferred_element_type=jnp.float32)
    raw = raw.reshape((local_experts, width, col_count))
    image = (raw * right_diag[:, None, :]).astype(jnp.bfloat16)
    column_term = (
        squared[:, None] * jnp.sum(jnp.square(image.astype(jnp.float32)), axis=1) / width - 1.0
    )
    column_level = jnp.max(jnp.abs(column_term), axis=1)
    groups = own_rows * lax.axis_size(SHARD) // own_rows

    def one_group(group):
        begin = group * own_rows
        picked = lax.dynamic_slice_in_dim(image, begin, own_rows, 1)
        window = lax.dynamic_slice_in_dim(image, begin // block * block, block, 1)
        return jnp.einsum("eic,ejc->iej", picked, window, preferred_element_type=jnp.float32)

    parts = lax.map(one_group, jnp.arange(groups, dtype=jnp.int32))
    gram = sum_by_axis(
        parts.reshape((own_rows * lax.axis_size(SHARD), local_experts, block)), SHARD
    )
    gram = jnp.transpose(gram, (1, 0, 2)) * (squared / (2 * FF))[:, None, None]
    my_index = lax.axis_index(SHARD)
    first_row = my_index * own_rows
    row_place = (first_row + lax.broadcasted_iota(jnp.int32, (own_rows, block), 0)) % block
    col_place = lax.broadcasted_iota(jnp.int32, (own_rows, block), 1)
    identity = jnp.where(col_place == row_place, 1.0, 0.0).astype(jnp.float32)
    upper_part = jnp.where((col_place >= row_place)[None, :, :], gram - identity[None, :, :], 0.0)
    row_level = jnp.max(jnp.abs(upper_part), axis=(1, 2))
    row_peak, column_peak = in_one((row_level, column_level), SHARD)
    steps = (upper_part / (row_peak + epsilon)[:, None, None]).astype(jnp.bfloat16)
    diag_block = lax.dynamic_slice_in_dim(whole, first_row // block * block, block, 1)
    moved = jnp.einsum("eik,ekj->eij", steps, diag_block, preferred_element_type=jnp.float32)
    new_factor = factor - step_rate * moved
    new_right = right_diag - step_rate * column_term / (column_peak + epsilon)[:, None] * right_diag
    return (new_factor, new_right)


def solution(mesh):
    torus = Mesh(
        mesh.devices.reshape(mesh.shape["expert"], 8, 4, 2),
        ("expert", "shard_0", "shard_1", "shard_2"),
    )
    return jax.shard_map(
        body,
        mesh=torus,
        in_specs=(
            P("expert", SHARD, None),
            P("expert", SHARD, None),
            P("expert", SHARD),
            P("expert"),
        ),
        out_specs=(P("expert", SHARD, None), P("expert", SHARD)),
        check_vma=False,
    )
```

profile of v0, /device:TPU:1, one launch (start us, length us, event | category | flops | bytes accessed | tf_op | source)
XLA Modules:
  0.0 385.5 jit_solution(12259285968247481593)
XLA Ops:
  8.1 11.3 %all-gather = bf16[4,32,512]{2,1,0:T(8,128)(2,1)} all-gather(bf16[1,32,512]{2,1,0:T(8,128)(2,1)S(1)} %convert_element_type.51), channel_id=2, replica_groups=mesh['expert'=4,'shard_0'=8,'shard_1'=4,'shard_2'=2] {'shard_1'}, dimensions={0}, use_global_device_ids=true | all-gather | bytes 163840 | tf_op jit(solution)/shard_map/all_gather | solution.py:53
  19.4 3.6 reshape.312
  23.0 1.2 copy.38
  24.4 9.7 %all_to_all.22 = bf16[32,2,1,32,448]{4,3,0,2,1:T(8,128)(2,1)S(1)} all-to-all(bf16[32,2,1,32,448]{4,3,0,2,1:T(8,128)(2,1)S(1)} %copy.39), channel_id=1, replica_groups=mesh['expert'=4,'shard_0'=8,'shard_1'=4,'shard_2'=2] {'shard_2'}, dimensions={1} | all-to-all | bytes 3670016 | tf_op jit(solution)/shard_map/all_to_all | solution.py:40
  34.2 1.6 copy.40
  35.8 9.1 %all-to-all-start.1 = ((bf16[32,2,1,32,448]{4,3,1,2,0:T(8,128)(2,1)}), bf16[32,2,1,32,448]{4,3,1,2,0:T(8,128)(2,1)}, u32[]{:S(2)}, u32[]{:S(2)}) async-start(bf16[32,2,1,32,448]{4,3,1,2,0:T(8,128)(2,1)} %copy.40), calls=%async_computation.1 | async-start | bytes 4194304 | tf_op jit(solution)/shard_map/all_to_all | solution.py:40
  44.9 21.0 %all-gather.6.cloned.1.call-done = bf16[32,32,512]{2,1,0:T(8,128)(2,1)} async-done(((bf16[4,32,512]{2,1,0:T(8,128)(2,1)}), bf16[32,32,512]{2,1,0:T(8,128)(2,1)}) %all-gather.6.cloned.1.call-update) | async-done | bytes 1048592 | tf_op jit(solution)/shard_map/all_gather | solution.py:53
  66.1 22.5 %all-gather.8.cloned.1.call-done = bf16[64,32,512]{2,1,0:T(8,128)(2,1)} async-done(((bf16[32,32,512]{2,1,0:T(8,128)(2,1)}), bf16[64,32,512]{2,1,0:T(8,128)(2,1)}) %all-gather.8.cloned.1.call-update) | async-done | bytes 2097168 | tf_op jit(solution)/shard_map/all_gather | solution.py:53
  88.5 1.7 copy.37
  90.3 8.6 %all-to-all-done.1 = bf16[32,2,1,32,448]{4,3,1,2,0:T(8,128)(2,1)} async-done(((bf16[32,2,1,32,448]{4,3,1,2,0:T(8,128)(2,1)}), bf16[32,2,1,32,448]{4,3,1,2,0:T(8,128)(2,1)}, u32[]{:S(2)}, u32[]{:S(2)}) %all-to-all-start.1) | async-done | bytes 1835040 | tf_op jit(solution)/shard_map/all_to_all | solution.py:40
  98.9 2.9 multiply_reduce_fusion
  101.8 4.3 %copy.42 = f32[4,512,448]{1,0,2:T(4,128)} copy(f32[4,512,448]{1,2,0:T(8,128)S(1)} %get-tuple-element.92) | data formatting | bytes 7340032 | tf_op jit(solution)/shard_map/ebik,ebkc->ebic/dot_general | solution.py:98
  106.1 5.5 %reshape.315 = f32[1,2048,448]{1,2,0:T(8,128)} reshape(f32[4,512,448]{1,0,2:T(4,128)} %copy.42) | data formatting | bytes 7340032 | tf_op jit(solution)/shard_map/reshape | solution.py:99
  111.6 3.6 multiply_convert_fusion.1
  115.2 2.8 copy.43
  118.0 138.5 %while.12 = (s32[]{:T(128)}, f32[64,32,1,512]{3,1,2,0:T(8,128)}, s32[64]{0:T(128)S(1)}, bf16[1,2048,448]{2,1,0:T(8,128)(2,1)S(1)}, s32[]{:T(128)}, /*index=5*/s3...) while((s32[]{:T(128)}, f32[64,32,1,512]{3,1,2,0:T(8,128)}, ...), condition=%wide.region_1.0_spmd, body=%wide.region_0.0_spmd.sunk | while | flops 14680088 | bytes 623474 | solution.py:113
  121.4 0.9 fusion.36
  123.6 0.9 fusion.36
  132.2 0.9 fusion.36
  134.4 0.9 fusion.36
  136.6 0.9 fusion.36
  140.9 0.9 fusion.36
  143.1 0.9 fusion.36
  145.2 0.9 fusion.36
  147.4 0.9 fusion.36
  149.6 0.9 fusion.36
  151.7 0.9 fusion.36
  156.1 0.9 fusion.36
  158.2 0.9 fusion.36
  166.9 0.9 fusion.36
  169.0 0.9 fusion.36
  179.8 0.9 fusion.36
  182.0 0.9 fusion.36
  186.3 0.9 fusion.36
  188.5 0.9 fusion.36
  190.7 0.9 fusion.36
  192.8 0.9 fusion.36
  197.1 0.9 fusion.36
  199.3 0.9 fusion.36
  201.5 0.9 fusion.36
  203.6 0.9 fusion.36
  208.0 0.9 fusion.36
  210.1 0.9 fusion.36
  216.6 0.9 fusion.36
  218.8 0.9 fusion.36
  221.0 0.9 fusion.36
  223.1 0.9 fusion.36
  225.3 0.9 fusion.36
  227.5 0.9 fusion.36
  229.6 0.9 fusion.36
  231.8 0.9 fusion.36
  233.9 0.9 fusion.36
  238.3 0.9 fusion.36
  251.2 0.9 fusion.36
  255.6 0.9 fusion.36
  256.5 54.2 %reduce-scatter.4.cloned.1.call-done = f32[256,1,512]{2,0,1:T(8,128)} async-done(((f32[2048,1,512]{2,0,1:T(8,128)}), f32[256,1,512]{2,0,1:T(8,128)}) %reduce-scatter.4.cloned.1.call-update) | async-done | bytes 524304 | tf_op jit(solution)/shard_map/reduce_scatter | solution.py:66
  312.0 4.0 %all-to-all-start.2 = ((s32[4,1,1]{2,1,0:T(1,128)}), s32[4,1,1]{2,1,0:T(1,128)S(1)}, u32[]{:S(2)}, u32[]{:S(2)}) async-start(s32[4,1,1]{2,1,0:T(1,128)} %broadcast_in_dim.51), calls=%async_computation.5 | async-start | bytes 4096 | tf_op jit(solution)/shard_map/all_to_all | solution.py:15
  316.0 17.7 %reduce-scatter.6.cloned.1.call-done = f32[64,1,512]{2,0,1:T(8,128)} async-done(((f32[256,1,512]{2,0,1:T(8,128)}), f32[64,1,512]{2,0,1:T(8,128)}) %reduce-scatter.6.cloned.1.call-update) | async-done | bytes 131088 | tf_op jit(solution)/shard_map/reduce_scatter | solution.py:66
  335.7 16.1 %reduce-scatter.8.cloned.1.call-done = f32[32,1,512]{2,0,1:T(8,128)} async-done(((f32[64,1,512]{2,0,1:T(8,128)}), f32[32,1,512]{2,0,1:T(8,128)}) %reduce-scatter.8.cloned.1.call-update) | async-done | bytes 65552 | tf_op jit(solution)/shard_map/reduce_scatter | solution.py:66
  351.8 1.5 fusion.12
  353.4 1.3 pad_maximum_fusion
  355.3 9.9 %all-to-all-start.3 = ((f32[64,1,2]{2,1,0:T(1,128)}), f32[64,1,2]{2,1,0:T(1,128)S(1)}, u32[]{:S(2)}, u32[]{:S(2)}) async-start(f32[64,1,2]{2,1,0:T(1,128)} %broadcast_in_dim.56), calls=%async_computation.6 | async-start | bytes 65536 | tf_op jit(solution)/shard_map/all_to_all | solution.py:15
  365.2 9.3 %all-to-all-done.3 = f32[64,1,2]{2,1,0:T(1,128)S(1)} async-done(((f32[64,1,2]{2,1,0:T(1,128)}), f32[64,1,2]{2,1,0:T(1,128)S(1)}, u32[]{:S(2)}, u32[]{:S(2)}) %all-to-all-start.3) | async-done | bytes 544 | tf_op jit(solution)/shard_map/all_to_all | solution.py:15
  377.0 2.0 fusion.7
  (120 shorter events, 64.7 us)
Async XLA Ops:
  7.2 58.8 %all-gather.6.cloned.1.call-start = ((), (), s32[]{:S(2)}) async-start(), calls=%async_computation.10 | async-start | bytes 1179648 | tf_op jit(solution)/shard_map/all_gather | solution.py:53
  35.8 63.1 %all-to-all-start.1 = ((bf16[32,2,1,32,448]{4,3,1,2,0:T(8,128)(2,1)}), bf16[32,2,1,32,448]{4,3,1,2,0:T(8,128)(2,1)}, u32[]{:S(2)}, u32[]{:S(2)}) async-start(bf16[32,2,1,32,448]{4,3,1,2,0:T(8,128)(2,1)} %copy.40), calls=%async_computation.1 | async-start | bytes 4194304 | tf_op jit(solution)/shard_map/all_to_all | solution.py:40
  44.9 43.7 %all-gather.8.cloned.1.call-start = ((), (), s32[]{:S(2)}) async-start(), calls=%async_computation.11 | async-start | bytes 3145728 | tf_op jit(solution)/shard_map/all_gather | solution.py:53
  66.0 244.8 %reduce-scatter.4.cloned.1.call-start = ((), (), s32[]{:S(2)}) async-start(), calls=%async_computation.7 | async-start | bytes 4718592 | tf_op jit(solution)/shard_map/reduce_scatter | solution.py:66
  88.5 10.3 %copy-start.2 = (f32[1,448]{1,0:T(1,128)S(1)}, f32[1,448]{1,0:T(1,128)}, u32[]{:S(2)}) copy-start(f32[1,448]{1,0:T(1,128)} %param.8) | copy-start | bytes 5380
  90.3 11.5 %copy-start = (bf16[2,8,4,1,32,512]{5,4,0,2,1,3:T(8,128)(2,1)}, bf16[2,8,4,1,32,512]{5,4,0,2,1,3:T(8,128)(2,1)S(1)}, u32[]{:S(2)}) copy-start(bf16[2,8,4,1,32,512]{5,4,0,2,1,3:T(8,128)(2,1)S(1)} %copy.37) | copy-start | bytes 6291460
  256.5 120.6 %copy-start.1 = (f32[1,32,512]{2,1,0:T(8,128)S(1)}, f32[1,32,512]{2,1,0:T(8,128)}, u32[]{:S(2)}) copy-start(f32[1,32,512]{2,1,0:T(8,128)} %param.7) | copy-start | bytes 196612
  256.5 77.2 %reduce-scatter.6.cloned.1.call-start = ((), (), s32[]{:S(2)}) async-start(), calls=%async_computation.8 | async-start | bytes 655360 | tf_op jit(solution)/shard_map/reduce_scatter | solution.py:66
  312.0 21.7 %all-to-all-start.2 = ((s32[4,1,1]{2,1,0:T(1,128)}), s32[4,1,1]{2,1,0:T(1,128)S(1)}, u32[]{:S(2)}, u32[]{:S(2)}) async-start(s32[4,1,1]{2,1,0:T(1,128)} %broadcast_in_dim.51), calls=%async_computation.5 | async-start | bytes 4096 | tf_op jit(solution)/shard_map/all_to_all | solution.py:15
  316.0 35.8 %reduce-scatter.8.cloned.1.call-start = ((), (), s32[]{:S(2)}) async-start(), calls=%async_computation.9 | async-start | bytes 196608 | tf_op jit(solution)/shard_map/reduce_scatter | solution.py:66
  355.3 19.2 %all-to-all-start.3 = ((f32[64,1,2]{2,1,0:T(1,128)}), f32[64,1,2]{2,1,0:T(1,128)S(1)}, u32[]{:S(2)}, u32[]{:S(2)}) async-start(f32[64,1,2]{2,1,0:T(1,128)} %broadcast_in_dim.56), calls=%async_computation.6 | async-start | bytes 65536 | tf_op jit(solution)/shard_map/all_to_all | solution.py:15
Sparse Core Ops, SparseCore 0:
  19.5 46.4 all-gather.5
  67.8 20.7 all-gather.7
  256.6 54.1 reduce-scatter.3
  313.2 20.4 reduce-scatter.5
  336.0 15.7 reduce-scatter.7
where the time goes:
time: 387 us; the launch traced here: 386 us
  waiting for transfers between devices  149 us (39%)
  matrix products  62.5 us (16%)
  local copies, waits for them, and re-layouts  60 us (16%)
  loops' own time  43.6 us (11%)
  starting transfers between devices  23.2 us (6%)
  blocking collectives  21.1 us (5%)
  between operations  16.5 us (4%)
  other arithmetic  9.29 us (2%)
    reduce_scatter x3, waiting for transfers between devices, sum_by_axis(): so_far = lax.psum_scatter(so_far, axis, scatter_dimension=0, tiled=True)  88 us
    dot_general x64, matrix products, one_group(): jnp.einsum('eic,ejc->iej', picked, window, preferred_element_type=jnp.flo...  57.6 us
    another operation x1, loops' own time, body(): parts = lax.map(one_group, jnp.arange(groups, dtype=jnp.int32))  43.6 us
    all_gather x2, waiting for transfers between devices, all_blocks(): parts = lax.all_gather(parts, axes[k], axis=0, tiled=True)  43.5 us
    dynamic_slice x64, local copies, waits for them, and re-layouts, body(): parts = lax.map(one_group, jnp.arange(groups, dtype=jnp.int32))  37.3 us
    all_to_all x2, starting transfers between devices, from_everyone(): lax.all_to_all(jnp.broadcast_to(shard[None], (size, *shard.shape)), axis,...  13.9 us
    all_gather x1, blocking collectives, all_blocks(): parts = lax.all_gather(parts, axes[k], axis=0, tiled=True)  11.3 us
    all_to_all x1, blocking collectives, moved_by_axis(): out = lax.all_to_all(out, axes[k], k, k, tiled=True)  9.74 us
  transfers between devices with their start and end apart: 8, of which 7 were waited for; matrix products, arithmetic and copies ran while one was open for 3% of the time, Pallas kernels for 0%

commit v1 on v0

--- a/solution.py
+++ b/solution.py
@@ -50,7 +50,13 @@
 def all_blocks(shard, axes, sequence):
     parts = shard[None]
     for k in sequence:
-        parts = lax.all_gather(parts, axes[k], axis=0, tiled=True)
+        inp = axes[k]
+        parts = jnp.concatenate(
+            lax.all_to_all(
+                jnp.stack([parts for _ in range(lax.axis_size(inp))], axis=0), inp, 0, 0
+            ),
+            0,
+        )
     held = [lax.axis_size(axes[k]) for k in reversed(sequence)]
     parts = parts.reshape(*held, *shard.shape)
     turned = sorted(range(len(sequence)), key=lambda place: sequence[len(sequence) - 1 - place])

time: 387 us -> 417 us (1.078)
  waiting for transfers between devices: 149 us -> 175 us
  starting transfers between devices: 23.2 us -> 33.7 us
  blocking collectives: 21.1 us -> 12.8 us
    all_gather x2 -> x0, waiting for transfers between devices: 43.5 us -> none  [all_blocks(): parts = lax.all_gather(parts, axes[k], axis=0, tiled=True)]
    all_to_all x1 -> x2, waiting for transfers between devices: 8.55 us -> 49.4 us  [moved_by_axis(): out = lax.all_to_all(out, axes[k], k, k, tiled=True)]
    all_to_all x0 -> x1, waiting for transfers between devices: none -> 27.7 us  [all_blocks(): lax.all_to_all(jnp.stack([parts for _ in range(lax.axis_size(inp))], axis...]
    all_gather x1 -> x0, blocking collectives: 11.3 us -> none  [all_blocks(): parts = lax.all_gather(parts, axes[k], axis=0, tiled=True)]
    all_to_all x0 -> x1, starting transfers between devices: none -> 7.89 us  [all_blocks(): lax.all_to_all(jnp.stack([parts for _ in range(lax.axis_size(inp))], axis...]
    all_to_all x1 -> x2, blocking collectives: 9.74 us -> 12.8 us  [all_blocks(): lax.all_to_all(jnp.stack([parts for _ in range(lax.axis_size(inp))], axis...]
    all_to_all x1 -> x2, starting transfers between devices: 9.12 us -> 11.8 us  [moved_by_axis(): out = lax.all_to_all(out, axes[k], k, k, tiled=True)]
  transfers between devices with their start and end apart: 8 -> 8, of which waited for: 7 -> 7; matrix products, arithmetic and copies ran while one was open for 3% -> 1% of each run, Pallas kernels for 0% -> 0%
where the time goes in v1:
time: 417 us; the launch traced here: 415 us
  waiting for transfers between devices  175 us (42%)
  matrix products  62.8 us (15%)
  local copies, waits for them, and re-layouts  62.1 us (15%)
  loops' own time  43.6 us (10%)
  starting transfers between devices  33.7 us (8%)
  between operations  16.5 us (4%)
  blocking collectives  12.8 us (3%)
  other arithmetic  8.64 us (2%)
    reduce_scatter x3, waiting for transfers between devices, sum_by_axis(): so_far = lax.psum_scatter(so_far, axis, scatter_dimension=0, tiled=True)  89 us
    dot_general x64, matrix products, one_group(): jnp.einsum('eic,ejc->iej', picked, window, preferred_element_type=jnp.flo...  57.3 us
    all_to_all x2, waiting for transfers between devices, moved_by_axis(): out = lax.all_to_all(out, axes[k], k, k, tiled=True)  49.4 us
    another operation x1, loops' own time, body(): parts = lax.map(one_group, jnp.arange(groups, dtype=jnp.int32))  43.6 us
    dynamic_slice x64, local copies, waits for them, and re-layouts, body(): parts = lax.map(one_group, jnp.arange(groups, dtype=jnp.int32))  37.3 us
    all_to_all x1, waiting for transfers between devices, all_blocks(): lax.all_to_all(jnp.stack([parts for _ in range(lax.axis_size(inp))], axis...  27.7 us
    all_to_all x2, starting transfers between devices, from_everyone(): lax.all_to_all(jnp.broadcast_to(shard[None], (size, *shard.shape)), axis,...  13.9 us
    all_to_all x2, blocking collectives, all_blocks(): lax.all_to_all(jnp.stack([parts for _ in range(lax.axis_size(inp))], axis...  12.8 us
  transfers between devices with their start and end apart: 8, of which 7 were waited for; matrix products, arithmetic and copies ran while one was open for 1% of the time, Pallas kernels for 0%

profile of v1, /device:TPU:1, one launch (start us, length us, event | category | flops | bytes accessed | tf_op | source)
XLA Modules:
  0.0 415.5 jit_solution(1416803030762261976)
XLA Ops:
  7.2 3.6 reshape.315
  10.8 1.2 copy.36
  11.9 1.6 copy.37
  13.5 7.1 %all-to-all-start.3 = ((bf16[32,2,1,32,448]{4,3,0,2,1:T(8,128)(2,1)}), bf16[32,2,1,32,448]{4,3,0,2,1:T(8,128)(2,1)S(1)}, u32[]{:S(2)}, u32[]{:S(2)}) async-start(bf16[32,2,1,32,448]{4,3,0,2,1:T(8,128)(2,1)} %copy.37), calls=%async_computation.3 | async-start | bytes 4194304 | tf_op jit(solution)/shard_map/all_to_all | solution.py:40
  20.6 2.5 all-to-all-done.3
  23.1 7.2 %all_to_all.37 = bf16[4,1,1,32,512]{4,3,2,1,0:T(8,128)(2,1)S(1)} all-to-all(bf16[4,1,1,32,512]{4,3,2,1,0:T(8,128)(2,1)S(1)} %stack.9), channel_id=1, replica_groups=mesh['expert'=4,'shard_0'=8,'shard_1'=4,'shard_2'=2] {'shard_1'}, dimensions={0} | all-to-all | bytes 262144 | tf_op jit(solution)/shard_map/all_to_all | solution.py:55
  30.4 1.1 stack.10
  31.5 7.9 %all-to-all-start.1 = ((bf16[8,4,1,32,512]{4,3,1,2,0:T(8,128)(2,1)}), bf16[8,4,1,32,512]{4,3,1,2,0:T(8,128)(2,1)S(1)}, u32[]{:S(2)}, u32[]{:S(2)}) async-start(bf16[8,4,1,32,512]{4,3,1,2,0:T(8,128)(2,1)} %stack.10), calls=%async_computation.1 | async-start | bytes 2097152 | tf_op jit(solution)/shard_map/all_to_all | solution.py:55
  39.3 1.5 copy.38
  40.8 27.7 %all-to-all-done.1 = bf16[8,4,1,32,512]{4,3,1,2,0:T(8,128)(2,1)S(1)} async-done(((bf16[8,4,1,32,512]{4,3,1,2,0:T(8,128)(2,1)}), bf16[8,4,1,32,512]{4,3,1,2,0:T(8,128)(2,1)S(1)}, u32[]{:S(2)}, u32[]{:S(2)}) %all-to-all-start.1) | async-done | bytes 1048608 | tf_op jit(solution)/shard_map/all_to_all | solution.py:55
  68.7 5.5 %all_to_all.38 = bf16[2,32,1,32,512]{4,3,1,2,0:T(8,128)(2,1)S(1)} all-to-all(bf16[2,32,1,32,512]{4,3,1,2,0:T(8,128)(2,1)S(1)} %pad_maximum_fusion), channel_id=1, replica_groups=mesh['expert'=4,'shard_0'=8,'shard_1'=4,'shard_2'=2] {'shard_2'}, dimensions={0} | all-to-all | bytes 4194304 | tf_op jit(solution)/shard_map/all_to_all | solution.py:55
  74.3 4.8 %all-to-all-start.4 = ((bf16[32,2,1,32,448]{4,3,1,2,0:T(8,128)(2,1)}), bf16[32,2,1,32,448]{4,3,1,2,0:T(8,128)(2,1)}, u32[]{:S(2)}, u32[]{:S(2)}) async-start(bf16[32,2,1,32,448]{4,3,1,2,0:T(8,128)(2,1)} %copy.38), calls=%async_computation.4 | async-start | bytes 4194304 | tf_op jit(solution)/shard_map/all_to_all | solution.py:40
  79.1 1.6 copy.35
  80.7 46.9 %all-to-all-done.4 = bf16[32,2,1,32,448]{4,3,1,2,0:T(8,128)(2,1)} async-done(((bf16[32,2,1,32,448]{4,3,1,2,0:T(8,128)(2,1)}), bf16[32,2,1,32,448]{4,3,1,2,0:T(8,128)(2,1)}, u32[]{:S(2)}, u32[]{:S(2)}) %all-to-all-start.4) | async-done | bytes 1835040 | tf_op jit(solution)/shard_map/all_to_all | solution.py:40
  127.5 3.6 multiply_reduce_fusion
  131.1 4.3 %copy.40 = f32[4,512,448]{1,0,2:T(4,128)} copy(f32[4,512,448]{1,2,0:T(8,128)S(1)} %get-tuple-element.92) | data formatting | bytes 7340032 | tf_op jit(solution)/shard_map/ebik,ebkc->ebic/dot_general | solution.py:104
  135.4 5.5 %reshape.318 = f32[1,2048,448]{1,2,0:T(8,128)} reshape(f32[4,512,448]{1,0,2:T(4,128)} %copy.40) | data formatting | bytes 7340032 | tf_op jit(solution)/shard_map/reshape | solution.py:105
  140.9 3.6 multiply_convert_fusion.1
  144.5 2.8 copy.41
  147.3 138.1 %while.12 = (s32[]{:T(128)}, f32[64,32,1,512]{3,1,2,0:T(8,128)}, s32[64]{0:T(128)S(1)}, bf16[1,2048,448]{2,1,0:T(8,128)(2,1)S(1)}, s32[]{:T(128)}, /*index=5*/s3...) while((s32[]{:T(128)}, f32[64,32,1,512]{3,1,2,0:T(8,128)}, ...), condition=%wide.region_1.0_spmd, body=%wide.region_0.0_spmd.sunk | while | flops 14680088 | bytes 623474 | solution.py:119
  155.0 0.9 fusion.36
  157.2 0.9 fusion.36
  159.4 0.9 fusion.36
  165.8 0.9 fusion.36
  170.2 0.9 fusion.36
  176.6 0.9 fusion.36
  178.8 0.9 fusion.36
  183.1 0.9 fusion.36
  185.3 0.9 fusion.36
  189.6 0.9 fusion.36
  193.9 0.9 fusion.36
  196.1 0.9 fusion.36
  198.2 0.9 fusion.36
  202.5 0.9 fusion.36
  204.7 0.9 fusion.36
  206.9 0.9 fusion.36
  213.3 0.9 fusion.36
  217.6 0.9 fusion.36
  221.9 0.9 fusion.36
  224.1 0.9 fusion.36
  226.3 0.9 fusion.36
  230.6 0.9 fusion.36
  232.8 0.9 fusion.36
  237.1 0.9 fusion.36
  239.2 0.9 fusion.36
  241.4 0.9 fusion.36
  245.7 0.9 fusion.36
  252.2 0.9 fusion.36
  258.6 0.9 fusion.36
  260.8 0.9 fusion.36
  269.4 0.9 fusion.36
  273.7 0.9 fusion.36
  275.9 0.9 fusion.36
  280.2 0.9 fusion.36
  282.4 0.9 fusion.36
  285.5 54.9 %reduce-scatter.4.cloned.1.call-done = f32[256,1,512]{2,0,1:T(8,128)} async-done(((f32[2048,1,512]{2,0,1:T(8,128)}), f32[256,1,512]{2,0,1:T(8,128)}) %reduce-scatter.4.cloned.1.call-update) | async-done | bytes 524304 | tf_op jit(solution)/shard_map/reduce_scatter | solution.py:72
  341.6 4.0 all-to-all-start.5
  345.6 17.8 %reduce-scatter.6.cloned.1.call-done = f32[64,1,512]{2,0,1:T(8,128)} async-done(((f32[256,1,512]{2,0,1:T(8,128)}), f32[64,1,512]{2,0,1:T(8,128)}) %reduce-scatter.6.cloned.1.call-update) | async-done | bytes 131088 | tf_op jit(solution)/shard_map/reduce_scatter | solution.py:72
  365.4 16.3 %reduce-scatter.8.cloned.1.call-done = f32[32,1,512]{2,0,1:T(8,128)} async-done(((f32[64,1,512]{2,0,1:T(8,128)}), f32[32,1,512]{2,0,1:T(8,128)}) %reduce-scatter.8.cloned.1.call-update) | async-done | bytes 65552 | tf_op jit(solution)/shard_map/reduce_scatter | solution.py:72
  381.7 1.6 fusion.12
  383.3 1.4 pad_maximum_fusion.1
  385.2 9.9 %all-to-all-start.6 = ((f32[64,1,2]{2,1,0:T(1,128)}), f32[64,1,2]{2,1,0:T(1,128)S(1)}, u32[]{:S(2)}, u32[]{:S(2)}) async-start(f32[64,1,2]{2,1,0:T(1,128)} %broadcast_in_dim.52), calls=%async_computation.9 | async-start | bytes 65536 | tf_op jit(solution)/shard_map/all_to_all | solution.py:15
  395.1 9.3 %all-to-all-done.6 = f32[64,1,2]{2,1,0:T(1,128)S(1)} async-done(((f32[64,1,2]{2,1,0:T(1,128)}), f32[64,1,2]{2,1,0:T(1,128)S(1)}, u32[]{:S(2)}, u32[]{:S(2)}) %all-to-all-start.6) | async-done | bytes 544 | tf_op jit(solution)/shard_map/all_to_all | solution.py:15
  407.0 2.0 fusion.7
  (119 shorter events, 67.2 us)
Async XLA Ops:
  13.5 7.1 %copy-start = (f32[1,32,512]{2,1,0:T(8,128)S(1)}, f32[1,32,512]{2,1,0:T(8,128)}, u32[]{:S(2)}) copy-start(f32[1,32,512]{2,1,0:T(8,128)} %param.7) | copy-start | bytes 196612
  13.5 9.6 %all-to-all-start.3 = ((bf16[32,2,1,32,448]{4,3,0,2,1:T(8,128)(2,1)}), bf16[32,2,1,32,448]{4,3,0,2,1:T(8,128)(2,1)S(1)}, u32[]{:S(2)}, u32[]{:S(2)}) async-start(bf16[32,2,1,32,448]{4,3,0,2,1:T(8,128)(2,1)} %copy.37), calls=%async_computation.3 | async-start | bytes 4194304 | tf_op jit(solution)/shard_map/all_to_all | solution.py:40
  31.5 37.1 %all-to-all-start.1 = ((bf16[8,4,1,32,512]{4,3,1,2,0:T(8,128)(2,1)}), bf16[8,4,1,32,512]{4,3,1,2,0:T(8,128)(2,1)S(1)}, u32[]{:S(2)}, u32[]{:S(2)}) async-start(bf16[8,4,1,32,512]{4,3,1,2,0:T(8,128)(2,1)} %stack.10), calls=%async_computation.1 | async-start | bytes 2097152 | tf_op jit(solution)/shard_map/all_to_all | solution.py:55
  74.3 53.3 %all-to-all-start.4 = ((bf16[32,2,1,32,448]{4,3,1,2,0:T(8,128)(2,1)}), bf16[32,2,1,32,448]{4,3,1,2,0:T(8,128)(2,1)}, u32[]{:S(2)}, u32[]{:S(2)}) async-start(bf16[32,2,1,32,448]{4,3,1,2,0:T(8,128)(2,1)} %copy.38), calls=%async_computation.4 | async-start | bytes 4194304 | tf_op jit(solution)/shard_map/all_to_all | solution.py:40
  79.0 261.3 %reduce-scatter.4.cloned.1.call-start = ((), (), s32[]{:S(2)}) async-start(), calls=%async_computation.10 | async-start | bytes 4718592 | tf_op jit(solution)/shard_map/reduce_scatter | solution.py:72
  79.1 48.5 %copy-start.1 = (f32[1,448]{1,0:T(1,128)S(1)}, f32[1,448]{1,0:T(1,128)}, u32[]{:S(2)}) copy-start(f32[1,448]{1,0:T(1,128)} %param.8) | copy-start | bytes 5380
  285.4 78.0 %reduce-scatter.6.cloned.1.call-start = ((), (), s32[]{:S(2)}) async-start(), calls=%async_computation.11 | async-start | bytes 655360 | tf_op jit(solution)/shard_map/reduce_scatter | solution.py:72
  341.6 21.9 %all-to-all-start.5 = ((s32[4,1,1]{2,1,0:T(1,128)}), s32[4,1,1]{2,1,0:T(1,128)S(1)}, u32[]{:S(2)}, u32[]{:S(2)}) async-start(s32[4,1,1]{2,1,0:T(1,128)} %broadcast_in_dim.47), calls=%async_computation.8 | async-start | bytes 4096 | tf_op jit(solution)/shard_map/all_to_all | solution.py:15
  345.6 36.1 %reduce-scatter.8.cloned.1.call-start = ((), (), s32[]{:S(2)}) async-start(), calls=%async_computation.12 | async-start | bytes 196608 | tf_op jit(solution)/shard_map/reduce_scatter | solution.py:72
  385.2 19.2 %all-to-all-start.6 = ((f32[64,1,2]{2,1,0:T(1,128)}), f32[64,1,2]{2,1,0:T(1,128)S(1)}, u32[]{:S(2)}, u32[]{:S(2)}) async-start(f32[64,1,2]{2,1,0:T(1,128)} %broadcast_in_dim.52), calls=%async_computation.9 | async-start | bytes 65536 | tf_op jit(solution)/shard_map/all_to_all | solution.py:15
Sparse Core Ops, SparseCore 0:
  285.6 54.7 reduce-scatter.3
  342.9 20.4 reduce-scatter.5
  365.9 15.7 reduce-scatter.7
